TPU v7x, 32 devices: a whole 2x2x4 slice. The times are simulated.
32 devices in a mesh: row: 8 (over y, x, core), col: 4 (over z).
Axes of the slice: x: 2, y: 2, z: 4, core: 2. Of those that a mesh axis runs over, the one named last changes fastest.
Arguments:
- choi: float32 [4, 2048, 1024], P(None, 'row', 'col'), may hold values from -0.5 to 8, as said below
Outputs:
- factored: float32 [4, 2048, 1024], P(None, 'row', 'col')
Inputs may be any that keep to these rules, and one draw needn't show every extreme that they name: `choi`: the leading 1024 x 1024 block of the matrix is symmetric with a positive diagonal, and its leading 2 * 256 square is positive definite.
All inputs are finite; a program needn't handle non-finite values.
Results may differ from a plain program's by a relative error of at most 0.0001.
Values sent between devices are 32-bit elements; how exact they have to be, the bound alone decides.
A program may use at most 64 MiB of HBM per device.

v0:
```python
import functools

import jax
import jax.numpy as jnp
from jax import lax
from jax.experimental import pallas as pl
from jax.experimental.pallas import tpu as pltpu
from jax.sharding import PartitionSpec as P

MESH = pl.DeviceIdType.MESH
HIGHEST = lax.Precision.HIGHEST
F32 = jnp.float32

TILES = ((0, 0, 0, 4), (1, 0, 1, 2), (1, 1, 1, 2), (0, None, 2, 2), (1, None, 2, 2))
MAX_CHUNKS = 4


def dot(a, b, ca=1, cb=0, precision=HIGHEST):
    return lax.dot_general(
        a, b, (((ca,), (cb,)), ((), ())), precision=precision, preferred_element_type=F32
    )


def split(x):
    high = x.astype(jnp.bfloat16)
    return high, (x - high.astype(F32)).astype(jnp.bfloat16)


def dot3(a, b):
    (ah, al), (bh, bl) = a, b

    def one(x, y):
        return jnp.dot(x, y, preferred_element_type=F32)

    return one(al, bh) + one(ah, bl) + one(ah, bh)


def pivot_rows(rows, lane, sub, first):
    n = rows.shape[1]
    wide = [jnp.broadcast_to(rows[j : j + 1, :], (8, n)) for j in range(8)]
    columns = [
        jnp.sum(jnp.where(lane == first + j, rows, 0.0), axis=1, keepdims=True) for j in range(8)
    ]
    columns = [jnp.broadcast_to(c, (8, n)) for c in columns]
    entry = [
        [jnp.broadcast_to(columns[j][i : i + 1, :], (8, n)) if j <= i else None for j in range(8)]
        for i in range(8)
    ]
    final = jnp.zeros((8, n), F32)
    for j in range(8):
        here = lane == first + j
        pivot = entry[j][j]
        inverse = 1.0 / pivot
        base = jnp.where(here, 1.0, wide[j])
        final = jnp.where(sub == j, base * lax.rsqrt(pivot), final)
        for i in range(j + 1, 8):
            scale = entry[i][j] * inverse
            wide[i] = jnp.where(here, 0.0, wide[i]) - scale * base
            for t in range(j + 1, i + 1):
                entry[i][t] = entry[i][t] - scale * entry[t][j]
    return final


def invert_factor(z_ref, between):
    n = z_ref.shape[0]
    lane = lax.broadcasted_iota(jnp.int32, (8, n), 1)
    sub = lax.broadcasted_iota(jnp.int32, (8, n), 0)
    all_lane = lax.broadcasted_iota(jnp.int32, (n, n), 1)
    all_row = lax.broadcasted_iota(jnp.int32, (n, n), 0)

    def group(g, carry):
        first = pl.multiple_of(8 * g, 8)
        final = pivot_rows(z_ref[pl.ds(first, 8), :], lane, sub, first)
        right = jnp.where((lane < first + 8) & (lane > first + sub), 0.0, final)
        left = jnp.where(lane >= first + 8, final, 0.0)
        change = dot(left, right, 0, 0)
        mine = (all_lane >= first) & (all_lane < first + 8) & (all_row >= first + 8)
        z_ref[...] = jnp.where(mine, 0.0, z_ref[...]) - change
        z_ref[pl.ds(first, 8), :] = right
        return carry

    quarter = n // 32
    for part in range(4):
        lax.fori_loop(part * quarter, (part + 1) * quarter, group, 0)
        between(part)
    z_ref[...] = jnp.where(all_lane <= all_row, z_ref[...], 0.0)


def kernel(
    rows, cols, a_ref, o_ref, tiles, slab, blocks, work, inverse, rhs, w_high, w_low,
    tile_send, tile_recv, slab_send, slab_recv,
):
    slots, size, _ = a_ref.shape
    half = size // 2
    r = lax.axis_index("row")
    c = lax.axis_index("col")
    bits = [k for k in range(rows.bit_length()) if (1 << k) < rows][::-1]

    def across(k):
        return r + (1 << k) * (1 - 2 * ((r // (1 << k)) % 2))

    barrier = pltpu.get_barrier_semaphore()
    for k in bits:
        pl.semaphore_signal(barrier, inc=1, device_id=(across(k), c), device_id_type=MESH)

    @pl.when(c > 0)
    def _():
        pl.semaphore_signal(barrier, inc=1, device_id=(r, c - 1), device_id_type=MESH)

    @pl.when(c < cols - 1)
    def _():
        pl.semaphore_signal(barrier, inc=1, device_id=(r, c + 1), device_id_type=MESH)

    peers = len(bits) + jnp.where(c > 0, 1, 0) + jnp.where(c < cols - 1, 1, 0)
    pl.semaphore_wait(barrier, peers)

    def place(t):
        root, owner_col, first_col, chunks = TILES[t]
        q = r if root == 0 else r + 1 - 2 * (r % 2)
        owner = (r == root) & ((c >= first_col) if owner_col is None else (c == owner_col))
        active = c >= first_col
        along = None
        if owner_col is not None:
            along = (r == root) & (c >= owner_col) & (c < cols - 1)
        down = [active & (q % (1 << (k + 1)) == 0) for k in bits]
        return chunks, owner, active & jnp.logical_not(owner), along, down

    def tile_copy(t, chunk, chunks, source, way, device):
        span = pl.ds(chunk * (size // chunks), size // chunks)
        return pltpu.make_async_remote_copy(
            src_ref=source.at[span],
            dst_ref=tiles.at[t, span],
            send_sem=tile_send.at[t, chunk, way],
            recv_sem=tile_recv.at[t, chunk],
            device_id=device,
            device_id_type=MESH,
        )

    def each_send(t, chunk, source, act):
        chunks, _, _, along, down = place(t)
        if along is not None:

            @pl.when(along)
            def _():
                act(tile_copy(t, chunk, chunks, source, 0, (r, c + 1)))

        for n, k in enumerate(bits):

            @pl.when(down[n])
            def _(n=n, k=k):
                act(tile_copy(t, chunk, chunks, source, n + 1, (across(k), c)))

    def slab_copy(which, s, source):
        return pltpu.make_async_remote_copy(
            src_ref=source.at[s],
            dst_ref=slab.at[which, s],
            send_sem=slab_send.at[which, s],
            recv_sem=slab_recv.at[which, s],
            device_id=(r, c + 1),
            device_id_type=MESH,
        )

    def needed(s):
        return (r >= 2) if s == 0 else (r >= 0)

    for t in range(len(TILES)):
        chunks, owner, _, _, _ = place(t)

        @pl.when(owner)
        def _(t=t, chunks=chunks):
            for chunk in range(chunks):
                each_send(t, chunk, a_ref.at[0], lambda copy: copy.start())

    def own_slab(which):
        for s in range(slots):

            @pl.when(needed(s))
            def _(s=s):
                slab_copy(which, s, a_ref).start()

    @pl.when(c == 0)
    def _():
        own_slab(0)

    if cols > 2:

        @pl.when((c == 1) & (r >= 2))
        def _():
            own_slab(1)

    for t in range(len(TILES)):

        @pl.when(place(t)[1])
        def _(t=t):
            tiles[t] = a_ref[0]

    def collect(t, which):
        chunks, _, receives, _, _ = place(t)

        @pl.when(receives & which)
        def _():
            for chunk in range(chunks):
                tile_copy(t, chunk, chunks, tiles.at[t], 0, (r, c)).wait_recv()
                each_send(t, chunk, tiles.at[t], lambda copy: copy.start())

    beyond = r + 1 - 2 * (r % 2)
    depth = sum((beyond // (1 << k)) % 2 for k in bits)
    for t in (3, 4, 0):
        collect(t, r >= 0)
    for t in (1, 2):
        collect(t, depth == 0)

    if cols > 2:

        @pl.when((c == 1) & (r < 2))
        def _():
            own_slab(1)

    def land(which, s):
        slab_copy(which, s, slab.at[which]).wait_recv()

    def pass_on(which, s):
        land(which, s)
        slab_copy(which, s, slab.at[which]).start()

    def arrive(position):
        s = position % slots
        which = 1 if position < slots else 0
        if position < slots:
            only = (c == 1) & needed(s)
            pl.when(only & (c < cols - 1))(lambda: pass_on(0, s))
            pl.when(only & (c == cols - 1))(lambda: land(0, s))
        if cols > 3:
            pl.when((c >= 2) & (c < cols - 1) & needed(s))(lambda: pass_on(which, s))

    pending = list(range(2 * slots))

    def take(count):
        for _ in range(min(count, len(pending))):
            arrive(pending.pop(0))

    def block_of(t, i, j):
        return tiles[t, i * half : (i + 1) * half, j * half : (j + 1) * half]

    for i in range(2):
        for j in range(i + 1):
            blocks[i, j] = block_of(0, i, j)

    @pl.when(c >= 1)
    def _():
        for i in range(2, 4):
            for j in range(2, i + 1):
                blocks[i, j] = jnp.zeros((half, half), F32)

    @pl.when(c >= 2)
    def _():
        for i in range(4):
            rhs[i] = tiles[3 + i // 2, (i % 2) * half : (i % 2 + 1) * half, :]

    during = ((1, 1), (1, 1), (0, 1), (1, 0))

    def between(k, part):
        if k == 0 and part == 0:
            collect(1, depth == 1)
        if k == 0 and part == 2:
            collect(1, depth == 2)
        if k == 0 and part == 3:
            collect(1, depth >= 3)
            collect(2, depth == 1)
        if k == 1 and part == 1:
            collect(2, depth == 2)
        if k == 1 and part == 3:
            collect(2, depth >= 3)
        if part == 1:
            take(during[k][0])

    take(2)
    for k in range(4):
        if k == 2:

            @pl.when(c >= 1)
            def _():
                for i in range(2, 4):
                    for j in range(2, i + 1):
                        blocks[i, j] = blocks[i, j] + block_of(2, i - 2, j - 2)

        def step(k=k):
            work[...] = blocks[k, k]
            invert_factor(work, lambda part: between(k, part))

        if k < 2:
            step()
        else:
            pl.when(c >= 1)(step)
        take(during[k][1])
        if k == 0:

            @pl.when(c >= 1)
            def _():
                for i in range(2, 4):
                    for j in range(2):
                        blocks[i, j] = block_of(1, i - 2, j)


        def finish(k=k):
            m = work[...]
            for j in range(k):
                blocks[k, j] = dot(m, blocks[k, j])
            targets = range(k + 1, 4)
            scaled = {i: dot(blocks[i, k], m, 1, 1) for i in targets}
            for i in targets:
                for j in range(k):
                    blocks[i, j] = blocks[i, j] - dot(scaled[i], blocks[k, j])
                blocks[i, k] = -dot(scaled[i], m)
                for j in range(k + 1, i + 1):
                    blocks[i, j] = blocks[i, j] - dot(scaled[i], scaled[j], 1, 1)
            blocks[k, k] = m

        if k < 2:

            @pl.when(c == 0)
            def _(k=k):
                m = work[...]
                if k == 0:
                    scaled = dot(blocks[1, 0], m, 1, 1)
                    blocks[1, 0] = -dot(scaled, m)
                    blocks[1, 1] = blocks[1, 1] - dot(scaled, scaled, 1, 1)
                else:
                    blocks[1, 0] = dot(m, blocks[1, 0])
                blocks[k, k] = m

        pl.when(c == 1)(finish)

        @pl.when(c >= 2)
        def _(k=k):
            m = work[...]
            scaled = {i: dot(blocks[i, k], m, 1, 1) for i in range(k + 1, 4)}
            for i in scaled:
                for j in range(k + 1, i + 1):
                    blocks[i, j] = blocks[i, j] - dot(scaled[i], scaled[j], 1, 1)
                blocks[i, k] = scaled[i]
            blocks[k, k] = m
            y = dot(m, rhs[k])
            for i in scaled:
                rhs[i] = rhs[i] - dot(scaled[i], y)
            rhs[k] = y

    def gather(n, i, j, zero):
        for x in range(2):
            for y in range(2):
                span = (slice(x * half, (x + 1) * half), slice(y * half, (y + 1) * half))
                if zero and y > x:
                    inverse[(n,) + span] = jnp.zeros((half, half), F32)
                else:
                    inverse[(n,) + span] = blocks[2 * i + x, 2 * j + y]

    lower = lax.broadcasted_iota(jnp.int32, (size, size), 0) >= lax.broadcasted_iota(
        jnp.int32, (size, size), 1
    )
    @pl.when(c == 0)
    def _():
        gather(0, 0, 0, True)

    @pl.when(c == 1)
    def _():
        gather(1, 1, 0, False)
        gather(2, 1, 1, True)

    @pl.when(c == 0)
    def _():
        for s in range(slots):
            o_ref[s] = dot(a_ref[s], inverse[0], 1, 1)

        @pl.when(r == 0)
        def _():
            o_ref[0] = jnp.where(lower, o_ref[0], 0.0)

    @pl.when(c == 1)
    def _():
        for s in range(slots):
            o_ref[s] = dot(a_ref[s], inverse[2], 1, 1)

        @pl.when(r == 1)
        def _():
            o_ref[0] = jnp.where(lower, o_ref[0] + dot(tiles[1], inverse[1], 1, 1), 0.0)

        @pl.when(r == 0)
        def _():
            o_ref[0] = jnp.zeros((size, size), F32)

    @pl.when(c >= 2)
    def _():
        w = {}
        for k in reversed(range(4)):
            x = rhs[k]
            for i in range(k + 1, 4):
                x = x - dot(blocks[i, k], w[i], 0, 0)
            w[k] = dot(blocks[k, k], x, 0, 0)
            high, low = split(w[k])
            span = slice((k % 2) * half, (k % 2 + 1) * half)
            w_high[k // 2, span, :] = high
            w_low[k // 2, span, :] = low

    @pl.when((c >= 2) & (r < 2))
    def _():
        o_ref[0] = a_ref[0]

    done = 2 * slots - len(pending)
    for position in range(2 * slots):
        if position >= done:
            take(1)
        s = position % slots
        if position < slots:

            @pl.when((c == 1) & needed(s))
            def _(s=s):
                o_ref[s] = o_ref[s] + dot(slab[0, s], inverse[1], 1, 1)

            @pl.when((c >= 2) & (c == cols - 1) & needed(s))
            def _(s=s):
                land(1, s)

            @pl.when((c >= 2) & needed(s))
            def _(s=s):
                o_ref[s] = a_ref[s] - dot3(split(slab[1, s]), (w_high[1], w_low[1]))

        else:

            @pl.when((c >= 2) & (c == cols - 1) & needed(s))
            def _(s=s):
                land(0, s)

            @pl.when((c >= 2) & needed(s))
            def _(s=s):
                o_ref[s] = o_ref[s] - dot3(split(slab[0, s]), (w_high[0], w_low[0]))

    for t in range(len(TILES)):
        for chunk in range(TILES[t][3]):
            each_send(t, chunk, tiles.at[t], lambda copy: copy.wait_send())
    for s in range(slots):

        @pl.when(needed(s) & (c < cols - 1))
        def _(s=s):
            slab_copy(0, s, a_ref).wait_send()

        @pl.when(needed(s) & (c >= 1) & (c < cols - 1))
        def _(s=s):
            slab_copy(1, s, a_ref).wait_send()


def solution(mesh):
    rows, cols = mesh.shape["row"], mesh.shape["col"]
    ways = rows.bit_length() + 1

    def body(choi):
        slots, size, _ = choi.shape
        half = size // 2
        vmem = pl.BlockSpec(memory_space=pltpu.VMEM)
        result = pl.pallas_call(
            functools.partial(kernel, rows, cols),
            out_shape=jax.ShapeDtypeStruct(choi.shape, F32),
            in_specs=[vmem],
            out_specs=vmem,
            scratch_shapes=[
                pltpu.VMEM((len(TILES), size, size), F32),
                pltpu.VMEM((2, slots, size, size), F32),
                pltpu.VMEM((4, 4, half, half), F32),
                pltpu.VMEM((half, half), F32),
                pltpu.VMEM((3, size, size), F32),
                pltpu.VMEM((4, half, size), F32),
                pltpu.VMEM((2, size, size), jnp.bfloat16),
                pltpu.VMEM((2, size, size), jnp.bfloat16),
                pltpu.SemaphoreType.DMA((len(TILES), MAX_CHUNKS, ways)),
                pltpu.SemaphoreType.DMA((len(TILES), MAX_CHUNKS)),
                pltpu.SemaphoreType.DMA((2, slots)),
                pltpu.SemaphoreType.DMA((2, slots)),
            ],
            compiler_params=pltpu.CompilerParams(collective_id=0, has_side_effects=True),
        )(choi)
        tile_row = jnp.arange(slots, dtype=jnp.int32) * rows + lax.axis_index("row")
        cleared = (lax.axis_index("col") >= 2) & (tile_row[:, None, None] < 2)
        return jnp.where(cleared, 0.0, result)

    return jax.shard_map(
        body,
        mesh=mesh,
        in_specs=(P(None, "row", "col"),),
        out_specs=P(None, "row", "col"),
        check_vma=False,
    )
```

profile of v0, /device:TPU:30, one launch (start us, length us, event | category | flops | bytes accessed | tf_op | source)
XLA Modules:
  0.0 70.2 jit_solution(3095143956779853427)
XLA Ops:
  0.0 67.8 %shard_map.17 = f32[4,256,256]{2,1,0:T(8,128)} custom-call(f32[4,256,256]{2,1,0:T(8,128)} %a_ref.1), custom_call_target="tpu_custom_call" | custom-call | tf_op jit(solution)/shard_map/pallas_call | solution.py:459
  67.8 2.4 %broadcast_select_fusion = f32[4,256,256]{2,1,0:T(8,128)} fusion(f32[4,256,256]{2,1,0:T(8,128)} %shard_map.17, pred[4]{0:T(512)(128)(4,1)S(1)} %compare_and_fusion), kind=kLoop, calls=%fused_computation | loop fusion | flops 262144 | bytes 2097156 | tf_op jit(solution)/shard_map/jit(_where)/select_n | solution.py:482
  (1 shorter events, 0.0 us)
where the time goes:
time: 70.9 us; the launch traced here: 70.2 us
  Pallas kernels  67.8 us (96%)
  other arithmetic  2.37 us (3%)
    pallas_call x1, Pallas kernels, body(): pl.pallas_call(functools.partial(kernel, rows, cols), out_shape=jax.Shape...  67.8 us
    select_n x1, other arithmetic, body(): return jnp.where(cleared, 0.0, result)  2.36 us

commit v1 on v0

v1 whole, which is shorter than its diff:
```python
import functools

import jax
import jax.numpy as jnp
from jax import lax
from jax.experimental import pallas as pl
from jax.experimental.pallas import tpu as pltpu
from jax.sharding import PartitionSpec as P

MESH = pl.DeviceIdType.MESH
HIGHEST = lax.Precision.HIGHEST
F32 = jnp.float32

PIECES = 4
ITEMS = (
    (0, 1, 0, 0, 0, 0, 2, 4, True),
    (0, 1, 0, 0, 0, 2, 2, 4, True),
    (0, 1, 0, 0, 0, 4, 2, 8, False),
    (0, 1, 0, 0, 0, 6, 2, 8, False),
    (1, 1, 1, 0, 1, 0, 2, 8, False),
    (1, 1, 1, 0, 1, 2, 2, 8, False),
    (1, 1, 1, 0, 1, 4, 2, 8, False),
    (1, 1, 1, 0, 1, 6, 2, 8, False),
    (2, 1, 1, 1, 1, 0, 4, 4, False),
    (2, 1, 1, 1, 1, 4, 2, 8, False),
    (2, 1, 1, 1, 1, 6, 2, 8, False),
    (3, 0, 0, None, 2, 0, 2, 8, False),
    (3, 0, 0, None, 2, 2, 2, 8, False),
    (3, 0, 0, None, 2, 4, 2, 8, False),
    (3, 0, 0, None, 2, 6, 2, 8, False),
    (4, 1, 1, None, 2, 0, 2, 8, False),
    (4, 1, 1, None, 2, 2, 2, 8, False),
    (4, 1, 1, None, 2, 4, 2, 8, False),
    (4, 1, 1, None, 2, 6, 2, 8, False),
)
FIRST, REST, BELOW, CORNER, TOP, NEXT = (
    (0, 1), (2, 3), (4, 5, 6, 7), (8, 9, 10), (11, 12, 13, 14), (15, 16, 17, 18),
)

TICKS = {
    "start": (4, 0),
    0: ((1, 0), (1, 1), (1, 1), (1, 1), (2, 2)),
    1: ((1, 1), (1, 1), (1, 1), (1, 1), (2, 2)),
    2: ((1, 1), (1, 1), (1, 1), (1, 1), (2, 1)),
    3: ((1, 1), (1, 1), (1, 1), (1, 1), (2, 2)),
}


def dot(a, b, ca=1, cb=0, precision=HIGHEST):
    return lax.dot_general(
        a, b, (((ca,), (cb,)), ((), ())), precision=precision, preferred_element_type=F32
    )


def split(x):
    high = x.astype(jnp.bfloat16)
    return high, (x - high.astype(F32)).astype(jnp.bfloat16)


def dot3(a, b):
    (ah, al), (bh, bl) = a, b

    def one(x, y):
        return jnp.dot(x, y, preferred_element_type=F32)

    return one(al, bh) + one(ah, bl) + one(ah, bh)


def pivot_rows(rows, lane, sub, first):
    n = rows.shape[1]
    wide = [jnp.broadcast_to(rows[j : j + 1, :], (8, n)) for j in range(8)]
    columns = [
        jnp.sum(jnp.where(lane == first + j, rows, 0.0), axis=1, keepdims=True) for j in range(8)
    ]
    columns = [jnp.broadcast_to(c, (8, n)) for c in columns]
    entry = [
        [jnp.broadcast_to(columns[j][i : i + 1, :], (8, n)) if j <= i else None for j in range(8)]
        for i in range(8)
    ]
    final = jnp.zeros((8, n), F32)
    for j in range(8):
        here = lane == first + j
        pivot = entry[j][j]
        inverse = 1.0 / pivot
        base = jnp.where(here, 1.0, wide[j])
        final = jnp.where(sub == j, base * lax.rsqrt(pivot), final)
        for i in range(j + 1, 8):
            scale = entry[i][j] * inverse
            wide[i] = jnp.where(here, 0.0, wide[i]) - scale * base
            for t in range(j + 1, i + 1):
                entry[i][t] = entry[i][t] - scale * entry[t][j]
    return final


def invert_factor(z_ref, between):
    n = z_ref.shape[0]
    lane = lax.broadcasted_iota(jnp.int32, (8, n), 1)
    sub = lax.broadcasted_iota(jnp.int32, (8, n), 0)
    all_lane = lax.broadcasted_iota(jnp.int32, (n, n), 1)
    all_row = lax.broadcasted_iota(jnp.int32, (n, n), 0)

    def group(g, carry):
        first = pl.multiple_of(8 * g, 8)
        final = pivot_rows(z_ref[pl.ds(first, 8), :], lane, sub, first)
        right = jnp.where((lane < first + 8) & (lane > first + sub), 0.0, final)
        left = jnp.where(lane >= first + 8, final, 0.0)
        change = dot(left, right, 0, 0)
        mine = (all_lane >= first) & (all_lane < first + 8) & (all_row >= first + 8)
        z_ref[...] = jnp.where(mine, 0.0, z_ref[...]) - change
        z_ref[pl.ds(first, 8), :] = right
        return carry

    quarter = n // 32
    for part in range(4):
        lax.fori_loop(part * quarter, (part + 1) * quarter, group, 0)
        between(part)
    z_ref[...] = jnp.where(all_lane <= all_row, z_ref[...], 0.0)


def kernel(
    rows, cols, a_ref, o_ref, tiles, slab, blocks, work, inverse, rhs, keep, w_high, w_low,
    tile_send, tile_recv, slab_send, slab_recv,
):
    slots, size, _ = a_ref.shape
    half = size // 2
    eighth = size // 8
    part_rows = size // PIECES
    r = lax.axis_index("row")
    c = lax.axis_index("col")
    bits = [k for k in range(rows.bit_length()) if (1 << k) < rows][::-1]
    leaders = list(range(2, rows, 2))
    far_leaders = [q for q in leaders if q & (q - 1)]

    def across(k):
        return r + (1 << k) * (1 - 2 * ((r // (1 << k)) % 2))

    barrier = pltpu.get_barrier_semaphore()
    peers = []

    def greet(when, device, count=1):
        def signal():
            pl.semaphore_signal(barrier, inc=1, device_id=device, device_id_type=MESH)

        if when is None:
            signal()
            peers.append(1)
        else:
            pl.when(when)(signal)
            peers.append(jnp.where(when, 1, 0))

    for k in bits:
        greet(None, (across(k), c))
    greet(c > 0, (r, c - 1))
    greet(c < cols - 1, (r, c + 1))
    for q in far_leaders:
        greet(r == 1, (q + 1, c))
        greet(r == q + 1, (1, c))
    pl.semaphore_wait(barrier, functools.reduce(lambda x, y: x + y, peers))

    def node(root):
        return r if root == 0 else r + 1 - 2 * (r % 2)

    def item_copy(item, source, way, device):
        tile, _, _, _, _, row0, height, width, _ = ITEMS[item]
        span = (pl.ds(row0 * eighth, height * eighth), pl.ds(0, width * eighth))
        return pltpu.make_async_remote_copy(
            src_ref=source.at[span],
            dst_ref=tiles.at[(tile,) + span],
            send_sem=tile_send.at[tile, way],
            recv_sem=tile_recv.at[item],
            device_id=device,
            device_id_type=MESH,
        )

    def owns(item):
        _, _, owner_row, owner_col, first_col = ITEMS[item][:5]
        return (r == owner_row) & ((c >= first_col) if owner_col is None else (c == owner_col))

    def routes(items, visit):
        for item in items:
            tile, root, owner_row, owner_col, first_col = ITEMS[item][:5]
            straight = ITEMS[item][8]
            q = node(root)
            if owner_row != root:
                visit(owns(item), 0, item)
            if owner_col is not None:
                visit((r == root) & (c >= owner_col) & (c < cols - 1), 1, item)
            if straight:
                for n in range(len(leaders)):
                    visit((c >= first_col) & (q == 0), 2 + len(bits) + n, item)
            for n, k in enumerate(bits):
                if straight and k > 0:
                    continue
                sends = (c >= first_col) & (q % (1 << (k + 1)) == 0)
                if k == 0 and owner_row != root:
                    sends = sends & ((q != 0) | (c != owner_col))
                visit(sends, 2 + n, item)

    def target(item, way):
        root = ITEMS[item][1]
        if way == 0:
            return (root, c)
        if way == 1:
            return (root, c + 1)
        if way < 2 + len(bits):
            return (across(bits[way - 2]), c)
        return (leaders[way - 2 - len(bits)] + root, c)

    def send(item, source, ways):
        def visit(when, way, item):
            if way in ways:
                pl.when(when)(lambda: item_copy(item, source, way, target(item, way)).start())

        routes((item,), visit)

    def depth_of(root):
        q = node(root)
        return sum((q // (1 << k)) % 2 for k in bits)

    onward = range(1, 2 + len(bits) + len(leaders))

    def launch(items):
        for item in items:
            ways = onward if ITEMS[item][1] == ITEMS[item][2] else (0,)
            pl.when(owns(item))(lambda item=item, ways=ways: send(item, a_ref.at[0], ways))

    def collect(items, low, high=99, which=True):
        for item in items:
            tile, root, _, _, first_col = ITEMS[item][:5]
            depth = depth_of(root)

            @pl.when(
                which
                & (c >= first_col)
                & jnp.logical_not(owns(item))
                & (depth >= low)
                & (depth <= high)
            )
            def _(item=item, tile=tile):
                item_copy(item, tiles.at[tile], 0, (r, c)).wait_recv()
                send(item, tiles.at[tile], onward)

    def slab_copy(which, s, p, source):
        span = pl.ds(p * part_rows, part_rows)
        return pltpu.make_async_remote_copy(
            src_ref=source.at[s, span],
            dst_ref=slab.at[which, s, span],
            send_sem=slab_send.at[which],
            recv_sem=slab_recv.at[which, s, p],
            device_id=(r, c + 1),
            device_id_type=MESH,
        )

    def own_slab(which, slots_from):
        for s in range(slots_from, slots):
            for p in range(PIECES):
                slab_copy(which, s, p, a_ref).start()

    launch(FIRST + REST)
    pl.when((c == 0) & (r >= 2))(lambda: own_slab(0, 0))
    if cols > 2:
        pl.when((c == 1) & (r >= 2))(lambda: own_slab(1, 0))

    for items in (FIRST, BELOW, CORNER, TOP, NEXT):

        @pl.when(owns(items[0]))
        def _(t=ITEMS[items[0]][0]):
            tiles[t] = a_ref[0]

    def land(which, s, p):
        slab_copy(which, s, p, slab.at[which]).wait_recv()

    def pass_on(which, s, p):
        land(which, s, p)
        slab_copy(which, s, p, slab.at[which]).start()

    def orders(first):
        return [(which, s, p) for which in (1, 0) for s in range(first, slots) for p in range(PIECES)]

    queues = {False: orders(0), True: orders(1)}
    done = {False: 0, True: 0}

    def serve_one(late):
        if done[late] >= len(queues[late]):
            return
        which, s, p = queues[late][done[late]]
        count = len(queues[late]) // 2
        mine = (r < 2) if late else (r >= 2)
        if done[late] < count and cols > 2:
            pl.when(mine & (c == 1))(lambda: pass_on(0, s, p))
        elif done[late] < count:
            pl.when(mine & (c == 1))(lambda: land(0, s, p))
        if cols > 3:
            pl.when(mine & (c >= 2) & (c < cols - 1))(lambda: pass_on(which, s, p))
        done[late] += 1

    def serve(main, late):
        for _ in range(main):
            serve_one(False)
        for _ in range(late):
            serve_one(True)

    def ensure(which, s, p):
        while queues[False].index((which, s, p)) >= done[False]:
            serve_one(False)
        if s >= 1:
            while queues[True].index((which, s, p)) >= done[True]:
                serve_one(True)

    collect(FIRST, 0)
    collect(REST, 0, 0)
    launch(BELOW)
    pl.when((c == 0) & (r == 1))(lambda: own_slab(0, 1))
    launch(CORNER)
    serve(*TICKS["start"])

    def between(k, part):
        if k == 0 and part == 0:
            collect(BELOW + CORNER, 0, 0, c == 1)
            if cols > 2:
                pl.when((c == 1) & (r < 2))(lambda: own_slab(1, 1))
        if k == 0 and part == 1:
            collect(REST, 1, 1)
            collect(BELOW + CORNER, 0, 0, c == 2)
        if k == 0 and part == 2:
            pl.when((c == 0) & (r == 0))(lambda: own_slab(0, 1))
            collect(REST, 2, 2)
            collect(BELOW + CORNER, 0, 0, c >= 3)
        if k == 0 and part == 3:
            collect(REST, 3)
            collect(BELOW[:2], 1, 1)
        if k == 1 and part == 0:
            collect(BELOW[2:], 1, 1)
            launch(TOP)
        if k == 1 and part == 1:
            collect(CORNER, 1, 1)
            collect(BELOW[:2], 2, 2)
        if k == 1 and part == 2:
            collect(BELOW[2:], 2, 2)
            launch(NEXT)
        if k == 1 and part == 3:
            collect(CORNER, 2, 2)
            collect(BELOW + CORNER, 3)
        if k == 2 and part == 0:
            collect(TOP + NEXT, 1, 1)
        if k == 2 and part == 2:
            collect(TOP + NEXT, 2, 2)
        if k == 2 and part == 3:
            collect(TOP + NEXT, 3)
        serve(*TICKS[k][part])

    low, high = slice(0, half), slice(half, size)

    def factor(k):
        invert_factor(work, lambda part: between(k, part))

    def halfway(n):
        m = work[...]
        inverse[n, low, low] = m
        inverse[n, low, high] = jnp.zeros((half, half), F32)
        scaled = dot(blocks[1], m, 1, 1)
        blocks[0] = dot(scaled, m)
        work[...] = blocks[2] - dot(scaled, scaled, 1, 1)

    def whole(n):
        m = work[...]
        inverse[n, high, low] = -dot(m, blocks[0])
        inverse[n, high, high] = m

    work[...] = tiles[0, low, low]
    factor(0)
    serve(*TICKS[0][4])
    blocks[1] = tiles[0, high, low]
    blocks[2] = tiles[0, high, high]
    halfway(0)
    factor(1)
    whole(0)
    serve(*TICKS[1][4])

    @pl.when(c >= 1)
    def _():
        beneath = dot(tiles[1], inverse[0], 1, 1)
        keep[0] = beneath
        corner = tiles[2] - dot(beneath, beneath, 1, 1)
        work[...] = corner[low, low]
        blocks[1] = corner[high, low]
        blocks[2] = corner[high, high]
        keep[1] = dot(beneath, inverse[0])

    lower = lax.broadcasted_iota(jnp.int32, (size, size), 0) >= lax.broadcasted_iota(
        jnp.int32, (size, size), 1
    )

    @pl.when(c == 0)
    def _():
        for s in range(slots):
            o_ref[s] = dot(a_ref[s], inverse[0], 1, 1)

        @pl.when(r == 0)
        def _():
            o_ref[0] = jnp.where(lower, o_ref[0], 0.0)

    @pl.when(c >= 1)
    def _():
        factor(2)
        serve(*TICKS[2][4])

        @pl.when(c >= 2)
        def _():
            y = dot(inverse[0], tiles[3])
            rhs[1] = tiles[4] - dot(keep[0], y)
            rhs[0] = dot(inverse[0], y, 0, 0)

        halfway(1)
        factor(3)
        whole(1)

    serve(*TICKS[3][4])
    for s in range(slots):
        for p in range(PIECES):
            ensure(1, s, p)

    @pl.when(c == 1)
    def _():
        rhs[0] = dot(inverse[1], keep[1])
        for s in range(slots):
            o_ref[s] = dot(a_ref[s], inverse[1], 1, 1)

        @pl.when(r == 1)
        def _():
            o_ref[0] = jnp.where(lower, o_ref[0] - dot(tiles[1], rhs[0], 1, 1), 0.0)

        @pl.when(r == 0)
        def _():
            o_ref[0] = jnp.zeros((size, size), F32)

        @pl.when(r >= 2)
        def _():
            o_ref[0] = o_ref[0] - dot(slab[0, 0], rhs[0], 1, 1)

        for s in range(1, slots):
            o_ref[s] = o_ref[s] - dot(slab[0, s], rhs[0], 1, 1)

    @pl.when(c >= 2)
    def _():
        w1 = dot(inverse[1], dot(inverse[1], rhs[1]), 0, 0)
        w_high[1], w_low[1] = split(w1)
        w_high[0], w_low[0] = split(rhs[0] - dot(keep[1], w1, 0, 0))

    @pl.when((c >= 2) & (r < 2))
    def _():
        o_ref[0] = jnp.zeros((size, size), F32)

    def trail(which, s, pieces):
        for p in pieces:
            ensure(which, s, p)
        span = slice(pieces[0] * part_rows, (pieces[-1] + 1) * part_rows)

        @pl.when((c >= 2) & ((r >= 2) if s == 0 else (r >= 0)))
        def _():
            @pl.when(c == cols - 1)
            def _():
                for p in pieces:
                    land(which, s, p)

            base = a_ref if which == 1 else o_ref
            w = (w_high[which], w_low[which])
            o_ref[s, span] = base[s, span] - dot3(split(slab[which, s, span]), w)

    everything = tuple(range(PIECES))
    for s in range(slots):
        trail(1, s, everything)
        serve(1, 1)
    for s in range(slots - 1):
        trail(0, s, everything)
        serve(1, 1)
    for p in everything:
        trail(0, slots - 1, (p,))

    def sent(source, sem):
        pltpu.make_async_remote_copy(
            src_ref=source,
            dst_ref=source,
            send_sem=sem,
            recv_sem=tile_recv.at[0],
            device_id=(r, c),
            device_id_type=MESH,
        ).wait_send()

    for items in (FIRST + REST, BELOW, CORNER, TOP, NEXT):
        area = {}
        tile = ITEMS[items[0]][0]
        routes(items, lambda when, way, item: area.setdefault(way, (when, []))[1].append(item))
        for way, (when, sent_items) in area.items():
            height = sum(ITEMS[i][6] * ITEMS[i][7] for i in sent_items) // 8
            pl.when(when)(
                lambda tile=tile, way=way, height=height: sent(
                    tiles.at[tile, pl.ds(0, height * eighth)], tile_send.at[tile, way]
                )
            )
    for low_row, mine in ((0, r >= 2), (1, r < 2)):
        for which in range(2):

            @pl.when(mine & (c >= which) & (c < cols - 1))
            def _(low_row=low_row, which=which):
                sent(slab.at[which, pl.ds(low_row, slots - low_row)], slab_send.at[which])


def solution(mesh):
    rows, cols = mesh.shape["row"], mesh.shape["col"]
    ways = 1 + rows.bit_length() + rows // 2

    def body(choi):
        slots, size, _ = choi.shape
        half = size // 2
        vmem = pl.BlockSpec(memory_space=pltpu.VMEM)
        result = pl.pallas_call(
            functools.partial(kernel, rows, cols),
            out_shape=pltpu.VMEM(choi.shape, F32),
            in_specs=[vmem],
            out_specs=vmem,
            scratch_shapes=[
                pltpu.VMEM((5, size, size), F32),
                pltpu.VMEM((2, slots, size, size), F32),
                pltpu.VMEM((3, half, half), F32),
                pltpu.VMEM((half, half), F32),
                pltpu.VMEM((2, size, size), F32),
                pltpu.VMEM((2, size, size), F32),
                pltpu.VMEM((2, size, size), F32),
                pltpu.VMEM((2, size, size), jnp.bfloat16),
                pltpu.VMEM((2, size, size), jnp.bfloat16),
                pltpu.SemaphoreType.DMA((5, ways)),
                pltpu.SemaphoreType.DMA((len(ITEMS),)),
                pltpu.SemaphoreType.DMA((2,)),
                pltpu.SemaphoreType.DMA((2, slots, PIECES)),
            ],
            compiler_params=pltpu.CompilerParams(collective_id=0, has_side_effects=True),
        )(choi)
        tile_row = jnp.arange(slots, dtype=jnp.int32) * rows + lax.axis_index("row")
        cleared = (lax.axis_index("col") >= 2) & (tile_row[:, None, None] < 2)
        return jnp.where(cleared, 0.0, result)

    return jax.shard_map(
        body,
        mesh=mesh,
        in_specs=(P(None, "row", "col"),),
        out_specs=P(None, "row", "col"),
        check_vma=False,
    )
```

time: 70.9 us -> 61.2 us (0.86)
  Pallas kernels: 67.8 us -> 59.6 us
  other arithmetic: 2.37 us -> 1.14 us
    pallas_call x1, Pallas kernels: 67.8 us -> 59.6 us  [body(): pl.pallas_call(functools.partial(kernel, rows, cols), out_shape=pltpu.VME...]
    select_n x1, other arithmetic: 2.36 us -> 1.13 us  [body(): return jnp.where(cleared, 0.0, result)]
where the time goes in v1:
time: 61.2 us; the launch traced here: 60.8 us
  Pallas kernels  59.6 us (97%)
  other arithmetic  1.14 us (2%)
    pallas_call x1, Pallas kernels, body(): pl.pallas_call(functools.partial(kernel, rows, cols), out_shape=pltpu.VME...  59.6 us

profile of v1, /device:TPU:30, one launch (start us, length us, event | category | flops | bytes accessed | tf_op | source)
XLA Modules:
  0.0 60.8 jit_solution(10299962335112049602)
XLA Ops:
  0.0 59.6 %shard_map.17 = f32[4,256,256]{2,1,0:T(8,128)S(1)} custom-call(f32[4,256,256]{2,1,0:T(8,128)} %a_ref.1), custom_call_target="tpu_custom_call" | custom-call | tf_op jit(solution)/shard_map/pallas_call | solution.py:517
  59.6 1.1 %broadcast_select_fusion = f32[4,256,256]{2,1,0:T(8,128)} fusion(f32[4,256,256]{2,1,0:T(8,128)S(1)} %shard_map.17, pred[4]{0:T(512)(128)(4,1)S(1)} %compare_and_fusion), kind=kLoop, calls=%fused_computation | loop fusion | flops 262144 | bytes 2097156 | tf_op jit(solution)/shard_map/jit(_where)/select_n | solution.py:541
  (1 shorter events, 0.0 us)

commit v2 on v1

--- a/solution.py
+++ b/solution.py
@@ -38,11 +38,28 @@
 )
 
 TICKS = {
-    "start": (4, 0),
-    0: ((1, 0), (1, 1), (1, 1), (1, 1), (2, 2)),
-    1: ((1, 1), (1, 1), (1, 1), (1, 1), (2, 2)),
-    2: ((1, 1), (1, 1), (1, 1), (1, 1), (2, 1)),
-    3: ((1, 1), (1, 1), (1, 1), (1, 1), (2, 2)),
+    "first": (3, 0, 0),
+    "start": (1, 0, 0),
+    0: (
+        (0, 1, 1, 0, 1, 1, 0, 1, 0, 1),
+        (0, 0, 0, 0, 0, 1, 0, 1, 0, 1),
+        (0, 0, 0, 2, 1, 0, 1, 1, 0, 0),
+    ),
+    1: (
+        (0, 1, 1, 0, 1, 1, 0, 1, 0, 1),
+        (0, 1, 1, 0, 1, 1, 0, 1, 0, 1),
+        (1, 1, 0, 1, 1, 0, 1, 1, 0, 1),
+    ),
+    2: (
+        (1, 0, 1, 1, 0, 1, 1, 0, 0, 1),
+        (1, 0, 1, 1, 0, 1, 1, 0, 0, 1),
+        (0, 1, 1, 0, 1, 1, 0, 1, 0, 0),
+    ),
+    3: (
+        (1, 0, 1, 1, 0, 1, 1, 0, 0, 1, 1, 0),
+        (0, 1, 1, 0, 1, 1, 0, 1, 0, 1, 0, 1),
+        (1, 1, 0, 1, 1, 0, 1, 1, 0, 2, 0, 0),
+    ),
 }
 
 
@@ -66,13 +83,18 @@
     return one(al, bh) + one(ah, bl) + one(ah, bh)
 
 
-def pivot_rows(rows, lane, sub, first):
+def pivot_rows(rows, rest, lane, sub, first):
     n = rows.shape[1]
     wide = [jnp.broadcast_to(rows[j : j + 1, :], (8, n)) for j in range(8)]
-    columns = [
-        jnp.sum(jnp.where(lane == first + j, rows, 0.0), axis=1, keepdims=True) for j in range(8)
-    ]
-    columns = [jnp.broadcast_to(c, (8, n)) for c in columns]
+
+    def spread(x):
+        columns = [
+            jnp.sum(jnp.where(lane == first + j, x, 0.0), axis=1, keepdims=True) for j in range(8)
+        ]
+        return [jnp.broadcast_to(c, (8, n)) for c in columns]
+
+    columns = spread(rows)
+    below = None if rest is None else spread(rest)
     entry = [
         [jnp.broadcast_to(columns[j][i : i + 1, :], (8, n)) if j <= i else None for j in range(8)]
         for i in range(8)
@@ -84,43 +106,53 @@
         inverse = 1.0 / pivot
         base = jnp.where(here, 1.0, wide[j])
         final = jnp.where(sub == j, base * lax.rsqrt(pivot), final)
+        if rest is not None:
+            scale = below[j] * inverse
+            rest = jnp.where(here, 0.0, rest) - scale * base
+            for t in range(j + 1, 8):
+                below[t] = below[t] - scale * entry[t][j]
         for i in range(j + 1, 8):
             scale = entry[i][j] * inverse
             wide[i] = jnp.where(here, 0.0, wide[i]) - scale * base
             for t in range(j + 1, i + 1):
                 entry[i][t] = entry[i][t] - scale * entry[t][j]
-    return final
+    return final, rest
 
 
 def invert_factor(z_ref, between):
     n = z_ref.shape[0]
     lane = lax.broadcasted_iota(jnp.int32, (8, n), 1)
     sub = lax.broadcasted_iota(jnp.int32, (8, n), 0)
+    wide_lane = lax.broadcasted_iota(jnp.int32, (16, n), 1)
+    wide_row = lax.broadcasted_iota(jnp.int32, (16, n), 0)
     all_lane = lax.broadcasted_iota(jnp.int32, (n, n), 1)
     all_row = lax.broadcasted_iota(jnp.int32, (n, n), 0)
 
-    def group(g, carry):
-        first = pl.multiple_of(8 * g, 8)
-        final = pivot_rows(z_ref[pl.ds(first, 8), :], lane, sub, first)
-        right = jnp.where((lane < first + 8) & (lane > first + sub), 0.0, final)
-        left = jnp.where(lane >= first + 8, final, 0.0)
-        change = dot(left, right, 0, 0)
-        mine = (all_lane >= first) & (all_lane < first + 8) & (all_row >= first + 8)
-        z_ref[...] = jnp.where(mine, 0.0, z_ref[...]) - change
-        z_ref[pl.ds(first, 8), :] = right
-        return carry
-
-    quarter = n // 32
-    for part in range(4):
-        lax.fori_loop(part * quarter, (part + 1) * quarter, group, 0)
-        between(part)
+    def panel(first):
+        last = first + 16
+        top, rest = pivot_rows(z_ref[first : first + 8, :], z_ref[first + 8 : last, :], lane, sub, first)
+        bottom, _ = pivot_rows(rest, None, lane, sub, first + 8)
+        final = jnp.concatenate([top, bottom], axis=0)
+        right = jnp.where((wide_lane < last) & (wide_lane > first + wide_row), 0.0, final)
+        z_ref[first:last, :] = right
+        if last < n:
+            left = jnp.where(wide_lane >= last, final, 0.0)
+            change = dot(left, right, 0, 0)
+            mine = (all_lane >= first) & (all_lane < last)
+            z_ref[last:, :] = jnp.where(mine, 0.0, z_ref[...])[last:] - change[last:]
+
+    for part in range(n // 16):
+        panel(16 * part)
+        between(part * 128 // n)
     z_ref[...] = jnp.where(all_lane <= all_row, z_ref[...], 0.0)
 
 
 def kernel(
-    rows, cols, a_ref, o_ref, tiles, slab, blocks, work, inverse, rhs, keep, w_high, w_low,
-    tile_send, tile_recv, slab_send, slab_recv,
+    rows, cols, x_ref, o_ref, a_ref, tiles, slab, blocks, work, inverse, rhs, keep, w_high, w_low,
+    load, tile_send, tile_recv, slab_send, slab_recv,
 ):
+    fill = pltpu.make_async_copy(x_ref, a_ref, load)
+    fill.start()
     slots, size, _ = a_ref.shape
     half = size // 2
     eighth = size // 8
@@ -155,6 +187,7 @@
     for q in far_leaders:
         greet(r == 1, (q + 1, c))
         greet(r == q + 1, (1, c))
+    fill.wait()
     pl.semaphore_wait(barrier, functools.reduce(lambda x, y: x + y, peers))
 
     def node(root):
@@ -166,7 +199,7 @@
         return pltpu.make_async_remote_copy(
             src_ref=source.at[span],
             dst_ref=tiles.at[(tile,) + span],
-            send_sem=tile_send.at[tile, way],
+            send_sem=tile_send.at[lanes.get((tile, way), 0)],
             recv_sem=tile_recv.at[item],
             device_id=device,
             device_id_type=MESH,
@@ -196,6 +229,9 @@
                     sends = sends & ((q != 0) | (c != owner_col))
                 visit(sends, 2 + n, item)
 
+    lanes = {}
+    routes(range(len(ITEMS)), lambda when, way, item: lanes.setdefault((ITEMS[item][0], way), len(lanes)))
+
     def target(item, way):
         root = ITEMS[item][1]
         if way == 0:
@@ -240,20 +276,27 @@
                 item_copy(item, tiles.at[tile], 0, (r, c)).wait_recv()
                 send(item, tiles.at[tile], onward)
 
+    def pieces(which, s):
+        spans = [(p * part_rows, part_rows) for p in range(PIECES)]
+        if which == 0 and s == slots - 1:
+            first, rows_left = spans.pop()
+            spans += [(first, rows_left // 2), (first + rows_left // 2, rows_left // 2)]
+        return range(len(spans)), spans
+
     def slab_copy(which, s, p, source):
-        span = pl.ds(p * part_rows, part_rows)
+        span = pl.ds(*pieces(which, s)[1][p])
         return pltpu.make_async_remote_copy(
             src_ref=source.at[s, span],
             dst_ref=slab.at[which, s, span],
             send_sem=slab_send.at[which],
-            recv_sem=slab_recv.at[which, s, p],
+            recv_sem=slab_recv.at[((1 - which) * slots + s) * PIECES + p],
             device_id=(r, c + 1),
             device_id_type=MESH,
         )
 
     def own_slab(which, slots_from):
         for s in range(slots_from, slots):
-            for p in range(PIECES):
+            for p in pieces(which, s)[0]:
                 slab_copy(which, s, p, a_ref).start()
 
     launch(FIRST + REST)
@@ -275,79 +318,91 @@
         slab_copy(which, s, p, slab.at[which]).start()
 
     def orders(first):
-        return [(which, s, p) for which in (1, 0) for s in range(first, slots) for p in range(PIECES)]
-
-    queues = {False: orders(0), True: orders(1)}
-    done = {False: 0, True: 0}
-
-    def serve_one(late):
-        if done[late] >= len(queues[late]):
+        return [
+            (which, s, p)
+            for which in (1, 0)
+            for s in range(first, slots)
+            for p in pieces(which, s)[0]
+        ]
+
+    queues = (orders(0), orders(1), orders(1))
+    done = [0, 0, 0]
+    members = (r >= 2, r == 0, r == 1)
+
+    def serve_one(n):
+        if done[n] >= len(queues[n]):
             return
-        which, s, p = queues[late][done[late]]
-        count = len(queues[late]) // 2
-        mine = (r < 2) if late else (r >= 2)
-        if done[late] < count and cols > 2:
-            pl.when(mine & (c == 1))(lambda: pass_on(0, s, p))
-        elif done[late] < count:
-            pl.when(mine & (c == 1))(lambda: land(0, s, p))
+        which, s, p = queues[n][done[n]]
+        order = [entry for entry in queues[n] if entry[0] == 0]
+        mine = members[n]
+        if done[n] < len(order):
+            act = pass_on if cols > 2 else land
+            pl.when(mine & (c == 1))(lambda: act(*order[done[n]]))
         if cols > 3:
             pl.when(mine & (c >= 2) & (c < cols - 1))(lambda: pass_on(which, s, p))
-        done[late] += 1
-
-    def serve(main, late):
-        for _ in range(main):
-            serve_one(False)
-        for _ in range(late):
-            serve_one(True)
+        done[n] += 1
+
+    def serve(*counts):
+        for n, count in enumerate(counts):
+            for _ in range(count):
+                serve_one(n)
 
     def ensure(which, s, p):
-        while queues[False].index((which, s, p)) >= done[False]:
-            serve_one(False)
-        if s >= 1:
-            while queues[True].index((which, s, p)) >= done[True]:
-                serve_one(True)
-
+        for n, queue in enumerate(queues):
+            while (which, s, p) in queue and queue.index((which, s, p)) >= done[n]:
+                serve_one(n)
+
+    serve(*TICKS["first"])
     collect(FIRST, 0)
-    collect(REST, 0, 0)
+    collect(REST, 0, 0, c == 0)
     launch(BELOW)
     pl.when((c == 0) & (r == 1))(lambda: own_slab(0, 1))
     launch(CORNER)
     serve(*TICKS["start"])
 
-    def between(k, part):
+    def tick(k, point):
+        serve(*(counts[point] for counts in TICKS[k]))
+
+    def between(k, point):
+        part = point / 2 - 0.5
         if k == 0 and part == 0:
+            collect(REST, 0, 0, (c >= 1) & (c <= 2))
             collect(BELOW + CORNER, 0, 0, c == 1)
             if cols > 2:
-                pl.when((c == 1) & (r < 2))(lambda: own_slab(1, 1))
+                pl.when((c == 1) & (r == 1))(lambda: own_slab(1, 1))
         if k == 0 and part == 1:
+            collect(REST, 0, 0, c >= 3)
             collect(REST, 1, 1)
             collect(BELOW + CORNER, 0, 0, c == 2)
         if k == 0 and part == 2:
+            if cols > 2:
+                pl.when((c == 1) & (r == 0))(lambda: own_slab(1, 1))
+            collect(REST, 2, 2)
+            collect(BELOW[:2], 0, 0, c >= 3)
+        if k == 0 and part == 3:
             pl.when((c == 0) & (r == 0))(lambda: own_slab(0, 1))
-            collect(REST, 2, 2)
-            collect(BELOW + CORNER, 0, 0, c >= 3)
-        if k == 0 and part == 3:
             collect(REST, 3)
+            collect(BELOW[2:], 0, 0, c >= 3)
+        if k == 1 and part == 0:
             collect(BELOW[:2], 1, 1)
-        if k == 1 and part == 0:
+        if k == 1 and part == 1:
+            collect(CORNER, 0, 0, c >= 3)
             collect(BELOW[2:], 1, 1)
             launch(TOP)
-        if k == 1 and part == 1:
+        if k == 1 and part == 2:
             collect(CORNER, 1, 1)
             collect(BELOW[:2], 2, 2)
-        if k == 1 and part == 2:
-            collect(BELOW[2:], 2, 2)
             launch(NEXT)
         if k == 1 and part == 3:
-            collect(CORNER, 2, 2)
+            collect(BELOW[2:] + CORNER, 2, 2)
             collect(BELOW + CORNER, 3)
-        if k == 2 and part == 0:
+        if k == 3 and part == 0:
             collect(TOP + NEXT, 1, 1)
-        if k == 2 and part == 2:
+        if k == 3 and part == 2:
             collect(TOP + NEXT, 2, 2)
-        if k == 2 and part == 3:
+        if k == 3 and part == 3:
             collect(TOP + NEXT, 3)
-        serve(*TICKS[k][part])
+        tick(k, point)
 
     low, high = slice(0, half), slice(half, size)
 
@@ -369,13 +424,14 @@
 
     work[...] = tiles[0, low, low]
     factor(0)
-    serve(*TICKS[0][4])
+    tick(0, 8)
     blocks[1] = tiles[0, high, low]
     blocks[2] = tiles[0, high, high]
     halfway(0)
+    tick(0, 9)
     factor(1)
     whole(0)
-    serve(*TICKS[1][4])
+    tick(1, 8)
 
     @pl.when(c >= 1)
     def _():
@@ -402,23 +458,44 @@
 
     @pl.when(c >= 1)
     def _():
+        tick(1, 9)
         factor(2)
-        serve(*TICKS[2][4])
-
-        @pl.when(c >= 2)
-        def _():
-            y = dot(inverse[0], tiles[3])
-            rhs[1] = tiles[4] - dot(keep[0], y)
-            rhs[0] = dot(inverse[0], y, 0, 0)
-
+        tick(2, 8)
         halfway(1)
+        tick(2, 9)
         factor(3)
+        pl.when(c == 1)(lambda: whole(1))
+
+    tick(3, 8)
+
+    @pl.when(c >= 2)
+    def _():
         whole(1)
-
-    serve(*TICKS[3][4])
+        y = dot(inverse[0], tiles[3])
+        rhs[0] = tiles[4] - dot(keep[0], y)
+        rhs[1] = dot(inverse[0], y, 0, 0)
+
+    tick(3, 9)
+
+    @pl.when(c >= 2)
+    def _():
+        w = dot(inverse[1], dot(inverse[1], rhs[0]), 0, 0)
+        rhs[0] = w
+        w_high[1], w_low[1] = split(w)
+
+    tick(3, 10)
+
+    @pl.when(c >= 2)
+    def _():
+        w_high[0], w_low[0] = split(rhs[1] - dot(keep[1], rhs[0], 0, 0))
+
+    tick(3, 11)
     for s in range(slots):
-        for p in range(PIECES):
+        for p in pieces(1, s)[0]:
             ensure(1, s, p)
+    for n, queue in enumerate(queues):
+        while done[n] < len([entry for entry in queue if entry[0] == 0]):
+            serve_one(n)
 
     @pl.when(c == 1)
     def _():
@@ -441,40 +518,37 @@
         for s in range(1, slots):
             o_ref[s] = o_ref[s] - dot(slab[0, s], rhs[0], 1, 1)
 
-    @pl.when(c >= 2)
-    def _():
-        w1 = dot(inverse[1], dot(inverse[1], rhs[1]), 0, 0)
-        w_high[1], w_low[1] = split(w1)
-        w_high[0], w_low[0] = split(rhs[0] - dot(keep[1], w1, 0, 0))
 
     @pl.when((c >= 2) & (r < 2))
     def _():
         o_ref[0] = jnp.zeros((size, size), F32)
 
-    def trail(which, s, pieces):
-        for p in pieces:
+    spans = {(which, s): pieces(which, s)[1] for which in range(2) for s in range(slots)}
+
+    def trail(which, s, ps):
+        for p in ps:
             ensure(which, s, p)
-        span = slice(pieces[0] * part_rows, (pieces[-1] + 1) * part_rows)
+        first, last = spans[which, s][ps[0]], spans[which, s][ps[-1]]
+        span = slice(first[0], last[0] + last[1])
 
         @pl.when((c >= 2) & ((r >= 2) if s == 0 else (r >= 0)))
         def _():
             @pl.when(c == cols - 1)
             def _():
-                for p in pieces:
+                for p in ps:
                     land(which, s, p)
 
             base = a_ref if which == 1 else o_ref
             w = (w_high[which], w_low[which])
             o_ref[s, span] = base[s, span] - dot3(split(slab[which, s, span]), w)
 
-    everything = tuple(range(PIECES))
     for s in range(slots):
-        trail(1, s, everything)
-        serve(1, 1)
+        trail(1, s, pieces(1, s)[0])
+        serve(1, 1, 1)
     for s in range(slots - 1):
-        trail(0, s, everything)
-        serve(1, 1)
-    for p in everything:
+        trail(0, s, pieces(0, s)[0])
+        serve(1, 1, 1)
+    for p in pieces(0, slots - 1)[0]:
         trail(0, slots - 1, (p,))
 
     def sent(source, sem):
@@ -495,7 +569,7 @@
             height = sum(ITEMS[i][6] * ITEMS[i][7] for i in sent_items) // 8
             pl.when(when)(
                 lambda tile=tile, way=way, height=height: sent(
-                    tiles.at[tile, pl.ds(0, height * eighth)], tile_send.at[tile, way]
+                    tiles.at[tile, pl.ds(0, height * eighth)], tile_send.at[lanes[tile, way]]
                 )
             )
     for low_row, mine in ((0, r >= 2), (1, r < 2)):
@@ -508,7 +582,7 @@
 
 def solution(mesh):
     rows, cols = mesh.shape["row"], mesh.shape["col"]
-    ways = 1 + rows.bit_length() + rows // 2
+    ways = 3 + 5 * (rows.bit_length() - 1) + rows // 2
 
     def body(choi):
         slots, size, _ = choi.shape
@@ -517,9 +591,10 @@
         result = pl.pallas_call(
             functools.partial(kernel, rows, cols),
             out_shape=pltpu.VMEM(choi.shape, F32),
-            in_specs=[vmem],
+            in_specs=[pl.BlockSpec(memory_space=pl.ANY)],
             out_specs=vmem,
             scratch_shapes=[
+                pltpu.VMEM(choi.shape, F32),
                 pltpu.VMEM((5, size, size), F32),
                 pltpu.VMEM((2, slots, size, size), F32),
                 pltpu.VMEM((3, half, half), F32),
@@ -529,10 +604,11 @@
                 pltpu.VMEM((2, size, size), F32),
                 pltpu.VMEM((2, size, size), jnp.bfloat16),
                 pltpu.VMEM((2, size, size), jnp.bfloat16),
-                pltpu.SemaphoreType.DMA((5, ways)),
+                pltpu.SemaphoreType.DMA,
+                pltpu.SemaphoreType.DMA((ways,)),
                 pltpu.SemaphoreType.DMA((len(ITEMS),)),
                 pltpu.SemaphoreType.DMA((2,)),
-                pltpu.SemaphoreType.DMA((2, slots, PIECES)),
+                pltpu.SemaphoreType.DMA((2 * slots * PIECES + 1,)),
             ],
             compiler_params=pltpu.CompilerParams(collective_id=0, has_side_effects=True),
         )(choi)

time: 61.2 us -> 54.3 us (0.89)
  Pallas kernels: 59.6 us -> 53 us
    pallas_call x1, Pallas kernels: 59.6 us -> 53 us  [body(): pl.pallas_call(functools.partial(kernel, rows, cols), out_shape=pltpu.VME...]
where the time goes in v2:
time: 54.3 us; the launch traced here: 54.1 us
  Pallas kernels  53 us (98%)
  other arithmetic  1.14 us (2%)
    pallas_call x1, Pallas kernels, body(): pl.pallas_call(functools.partial(kernel, rows, cols), out_shape=pltpu.VME...  53 us
    select_n x1, other arithmetic, body(): return jnp.where(cleared, 0.0, result)  1.13 us

profile of v2, /device:TPU:30, one launch (start us, length us, event | category | flops | bytes accessed | tf_op | source)
XLA Modules:
  0.0 54.1 jit_solution(1777854516768524665)
XLA Ops:
  0.0 53.0 %shard_map.17 = f32[4,256,256]{2,1,0:T(8,128)S(1)} custom-call(f32[4,256,256]{2,1,0:T(8,128)} %x_ref.1), custom_call_target="tpu_custom_call" | custom-call | tf_op jit(solution)/shard_map/pallas_call | solution.py:591
  53.0 1.1 %broadcast_select_fusion = f32[4,256,256]{2,1,0:T(8,128)} fusion(f32[4,256,256]{2,1,0:T(8,128)S(1)} %shard_map.17, pred[4]{0:T(512)(128)(4,1)S(1)} %compare_and_fusion), kind=kLoop, calls=%fused_computation | loop fusion | flops 262144 | bytes 2097156 | tf_op jit(solution)/shard_map/jit(_where)/select_n | solution.py:617
  (1 shorter events, 0.0 us)

commit v3 on v2

--- a/solution.py
+++ b/solution.py
@@ -396,12 +396,18 @@
         if k == 1 and part == 3:
             collect(BELOW[2:] + CORNER, 2, 2)
             collect(BELOW + CORNER, 3)
+        if k == 2 and part == 1:
+            collect(TOP, 1, 1)
+        if k == 2 and part == 3:
+            collect(TOP, 2, 2)
         if k == 3 and part == 0:
-            collect(TOP + NEXT, 1, 1)
+            collect(NEXT, 1, 1)
+        if k == 3 and part == 1:
+            collect(TOP, 3)
         if k == 3 and part == 2:
-            collect(TOP + NEXT, 2, 2)
+            collect(NEXT, 2, 2)
         if k == 3 and part == 3:
-            collect(TOP + NEXT, 3)
+            collect(NEXT, 3)
         tick(k, point)
 
     low, high = slice(0, half), slice(half, size)

time: 54.3 us -> 53.6 us (0.987)
  Pallas kernels: 53 us -> 52.2 us
    pallas_call x1, Pallas kernels: 53 us -> 52.2 us  [body(): pl.pallas_call(functools.partial(kernel, rows, cols), out_shape=pltpu.VME...]
where the time goes in v3:
time: 53.6 us; the launch traced here: 53.3 us
  Pallas kernels  52.2 us (97%)
  other arithmetic  1.14 us (2%)
    pallas_call x1, Pallas kernels, body(): pl.pallas_call(functools.partial(kernel, rows, cols), out_shape=pltpu.VME...  52.2 us
    select_n x1, other arithmetic, body(): return jnp.where(cleared, 0.0, result)  1.13 us

profile of v3, /device:TPU:30, one launch (start us, length us, event | category | flops | bytes accessed | tf_op | source)
XLA Modules:
  0.0 53.3 jit_solution(3366162372743405078)
XLA Ops:
  0.0 52.2 %shard_map.17 = f32[4,256,256]{2,1,0:T(8,128)S(1)} custom-call(f32[4,256,256]{2,1,0:T(8,128)} %x_ref.1), custom_call_target="tpu_custom_call" | custom-call | tf_op jit(solution)/shard_map/pallas_call | solution.py:597
  52.2 1.1 %broadcast_select_fusion = f32[4,256,256]{2,1,0:T(8,128)} fusion(f32[4,256,256]{2,1,0:T(8,128)S(1)} %shard_map.17, pred[4]{0:T(512)(128)(4,1)S(1)} %compare_and_fusion), kind=kLoop, calls=%fused_computation | loop fusion | flops 262144 | bytes 2097156 | tf_op jit(solution)/shard_map/jit(_where)/select_n | solution.py:623
  (1 shorter events, 0.0 us)
